TPU v7x, 32 devices: a whole 2x2x4 slice. The times are simulated.
32 devices in a mesh: gx: 8 (over y, x, core), wa: 4 (over z).
Axes of the slice: x: 2, y: 2, z: 4, core: 2. Of those that a mesh axis runs over, the one named last changes fastest.
Arguments:
- warm_field: float32 [64, 2, 128, 2048], P('wa', None, 'gx'), may hold values from -1.8 to 1.8
- warm_adjoint: float32 [64, 2, 128, 2048], P('wa', None, 'gx'), may hold values from -1.8 to 1.8
- permittivity: float32 [128, 2048], P('gx'), may hold values from 1 to 12
- design_mask: int32 [128, 2048], P('gx'), may hold values 0 or 1
- source_row: int32 [64], P('wa'), may hold values from 0 to 127
- monitor_row: int32 [64], P('wa'), may hold values from 0 to 127
- wavenumber: float32 [64], P('wa'), may hold values from 0.02 to 0.08
- bloch_phase: float32 [64], P('wa'), may hold values from -3.140625 to 3.140625
- source_profile: float32 [64, 2, 2048], P('wa'), may hold values from -24 to 24
- monitor_profile: float32 [64, 2, 2048], P('wa'), may hold values from -4 to 4
Outputs:
- forward_field: float32 [64, 2, 128, 2048], P('wa', None, 'gx')
- adjoint_field: float32 [64, 2, 128, 2048], P('wa', None, 'gx')
- gradient: float32 [128, 2048], P('gx')
All inputs are finite; a program needn't handle non-finite values. No bound on the sum of `design_mask` on one device may be relied on, other than what follows from the above.
Results may differ from a plain program's by a relative error of at most 0.0003.
Values sent between devices are 32-bit elements; how exact they have to be, the bound alone decides.
A program may use at most 128 MiB of HBM per device.

v0:
```python
import functools

import jax
import jax.numpy as jnp
from jax import lax
from jax.experimental import pallas as pl
from jax.experimental.pallas import tpu as pltpu
from jax.sharding import PartitionSpec as P

floor_share = 0.5
REACH = 3
TILE = 8
SUMS = 16
VMEM_LIMIT = 48 * 1024 * 1024


def stencil(u, d, rows):
    total, width = u.shape
    col = lax.broadcasted_iota(jnp.int32, (total, width), 1)
    after = jnp.where(col == width - 1, 0.0, pltpu.roll(u, width - 1, 1))
    before = jnp.where(col == 0, 0.0, pltpu.roll(u, 1, 1))
    above = pltpu.roll(u, total - 1, 0)
    below = pltpu.roll(u, 1, 0)
    return (d * u - (above + below + after + before))[:rows]


def lay_out(ext, x_ref, hi_ref, lo_ref, scal, wave, sign):
    rows = x_ref.shape[2]
    ext[:, :rows] = x_ref[0]
    low_c, low_s, high_c, high_s = (scal[wave, i] for i in range(1, 5))
    hi_re, hi_im = hi_ref[0, 0], hi_ref[0, 1]
    lo_re, lo_im = lo_ref[0, 0], lo_ref[0, 1]
    high_s = sign * high_s
    low_s = sign * low_s
    ext[0, rows : rows + REACH] = high_c * hi_re - high_s * hi_im
    ext[1, rows : rows + REACH] = high_s * hi_re + high_c * hi_im
    ext[0, rows + TILE - REACH :] = low_c * lo_re - low_s * lo_im
    ext[1, rows + TILE - REACH :] = low_s * lo_re + low_c * lo_im


def clear_gap(ext, rows):
    @pl.when(pl.program_id(0) == 0)
    def _():
        ext[:, rows:] = jnp.zeros((2, TILE, ext.shape[2]), jnp.float32)


def residual(ext, res, d, spot, side_re, side_im):
    total = ext.shape[1]
    for part in range(2):
        res[part] = -stencil(ext[part], d, total)

    @pl.when(spot >= 0)
    def _():
        res[0, pl.ds(spot, 1)] = res[0, pl.ds(spot, 1)] + side_re
        res[1, pl.ds(spot, 1)] = res[1, pl.ds(spot, 1)] + side_im


def fold(cells):
    width = cells.shape[1]
    acc = cells[:, :128]
    for start in range(128, width, 128):
        acc = acc + cells[:, start : start + 128]
    return jnp.sum(acc, axis=0, keepdims=True)


def put_dots(out, r, v, w):
    out[0, 0:1] = fold(r[0] * r[0] + r[1] * r[1])
    out[0, 1:2] = fold(r[0] * v[0] + r[1] * v[1])
    out[0, 2:3] = fold(r[0] * v[1] - r[1] * v[0])
    out[0, 3:4] = fold(v[0] * v[0] + v[1] * v[1])
    out[0, 4:5] = fold(w[0] * r[0] + w[1] * r[1])
    out[0, 5:6] = fold(w[0] * r[1] - w[1] * r[0])
    out[0, 6:7] = fold(w[0] * v[0] + w[1] * v[1])
    out[0, 7:8] = fold(w[0] * v[1] - w[1] * v[0])
    out[0, 8:9] = fold(w[0] * w[0] + w[1] * w[1])


def images(res, d, inv, rows, deep, keep=None):
    total = res.shape[1]
    z = [res[part] * inv for part in range(2)]
    v = [stencil(z[part], d, total if deep else rows) for part in range(2)]
    if not deep:
        return [u[:rows] for u in z], v, None
    y = [v[part] * inv for part in range(2)]
    if keep is not None:
        keep(z, y)
    w = [stencil(y[part], d, rows) for part in range(2)]
    return z, [u[:rows] for u in v], w


def side_row(profile_re, profile_im, scal, wave, slot):
    turn_c, turn_s = scal[wave, slot], scal[wave, slot + 1]
    return (
        turn_c * profile_re - turn_s * profile_im,
        turn_s * profile_re + turn_c * profile_im,
    )


def first_pass(
    scal, spots, eps, x_ref, hi_ref, lo_ref, src_ref, mon_ref, out, ext, res, zed, yed
):
    wave = pl.program_id(0)
    rows = x_ref.shape[2]
    clear_gap(ext, rows)
    lay_out(ext, x_ref, hi_ref, lo_ref, scal, wave, 1.0)
    d = 4.0 - scal[wave, 0] * eps[...]
    inv = 1.0 / d
    side_re, side_im = side_row(src_ref[0, 0:1], src_ref[0, 1:2], scal, wave, 5)
    residual(ext, res, d, spots[wave, 0], side_re, side_im)

    def keep(z, y):
        for part in range(2):
            zed[part] = z[part][:rows]
            yed[part] = y[part][:rows]

    z, v, w = images(res, d, inv, rows, True, keep)
    r = [res[part, :rows] for part in range(2)]
    put_dots(out, r, v, w)
    out[0, 9:SUMS] = jnp.zeros((SUMS - 9, 128), jnp.float32)
    mon = spots[wave, 1]

    @pl.when((mon >= 0) & (mon < rows))
    def _():
        m_re, m_im = mon_ref[0, 0:1], mon_ref[0, 1:2]
        for slot, held in ((9, ext), (11, zed), (13, yed)):
            f_re, f_im = held[0, pl.ds(mon, 1)], held[1, pl.ds(mon, 1)]
            out[0, slot : slot + 1] = fold(m_re * f_re + m_im * f_im)
            out[0, slot + 1 : slot + 2] = fold(m_re * f_im - m_im * f_re)


def step_result(ext, res, z, v, inv, coef, wave, rows):
    a_re, a_im, o_re, o_im = (coef[wave, i] for i in range(4))
    x = [ext[part, :rows] for part in range(2)]
    r = [res[part, :rows] for part in range(2)]
    inv = inv[:rows]
    y_re = (r[0] - (a_re * v[0] - a_im * v[1])) * inv
    y_im = (r[1] - (a_re * v[1] + a_im * v[0])) * inv
    out_re = x[0] + (a_re * z[0] - a_im * z[1]) + (o_re * y_re - o_im * y_im)
    out_im = x[1] + (a_re * z[1] + a_im * z[0]) + (o_re * y_im + o_im * y_re)
    return out_re, out_im


def adjoint_row(mon_ref, coef, scal, wave):
    over_re, over_im = coef[wave, 4], coef[wave, 5]
    m_re, m_im = mon_ref[0, 0:1], mon_ref[0, 1:2]
    adj_re = over_re * m_re - over_im * m_im
    adj_im = -(over_re * m_im + over_im * m_re)
    return side_row(adj_re, adj_im, scal, wave, 7)


def second_pass(
    scal, spots, coef, eps, x_ref, hi_ref, lo_ref, ax_ref, ahi_ref, alo_ref, src_ref, mon_ref,
    fwd, out, ext, res, aext, ares,
):
    wave = pl.program_id(0)
    rows = x_ref.shape[2]
    clear_gap(ext, rows)
    clear_gap(aext, rows)
    d = 4.0 - scal[wave, 0] * eps[...]
    inv = 1.0 / d
    lay_out(ext, x_ref, hi_ref, lo_ref, scal, wave, 1.0)
    side_re, side_im = side_row(src_ref[0, 0:1], src_ref[0, 1:2], scal, wave, 5)
    residual(ext, res, d, spots[wave, 0], side_re, side_im)
    z, v, _ = images(res, d, inv, rows, False)
    fwd[0, 0], fwd[0, 1] = step_result(ext, res, z, v, inv, coef, wave, rows)

    lay_out(aext, ax_ref, ahi_ref, alo_ref, scal, wave, -1.0)
    adj_re, adj_im = adjoint_row(mon_ref, coef, scal, wave)
    residual(aext, ares, d, spots[wave, 1], adj_re, adj_im)
    z, v, w = images(ares, d, inv, rows, True)
    put_dots(out, [ares[part, :rows] for part in range(2)], v, w)
    out[0, 9:SUMS] = jnp.zeros((SUMS - 9, 128), jnp.float32)


def third_pass(
    scal, spots, coef, acoef, eps, ax_ref, ahi_ref, alo_ref, mon_ref, fwd, adj, grad, aext, ares
):
    wave = pl.program_id(0)
    rows = ax_ref.shape[2]
    clear_gap(aext, rows)
    d = 4.0 - scal[wave, 0] * eps[...]
    inv = 1.0 / d
    lay_out(aext, ax_ref, ahi_ref, alo_ref, scal, wave, -1.0)
    adj_re, adj_im = adjoint_row(mon_ref, coef, scal, wave)
    residual(aext, ares, d, spots[wave, 1], adj_re, adj_im)
    z, v, _ = images(ares, d, inv, rows, False)
    out_re, out_im = step_result(aext, ares, z, v, inv, acoef, wave, rows)
    adj[0, 0] = out_re
    adj[0, 1] = out_im
    term = (2.0 * scal[wave, 0]) * (out_re * fwd[0, 0] - out_im * fwd[0, 1])

    @pl.when(wave == 0)
    def _():
        grad[...] = term

    @pl.when(wave > 0)
    def _():
        grad[...] = grad[...] + term


def greet(axis, count, me):
    barrier = pltpu.get_barrier_semaphore()
    for hop in range(1, count):
        pl.semaphore_signal(
            barrier, inc=1, device_id={axis: lax.rem(me + hop, count)},
            device_id_type=pl.DeviceIdType.MESH,
        )
    pl.semaphore_wait(barrier, count - 1)


def sum_kernel(count, with_overlap, parts, coef, mine, got, send_sem, recv_sem):
    me = lax.axis_index("gx")
    local_sum = jnp.sum(parts[...], axis=-1)
    mine[...] = local_sum
    greet("gx", count, me)

    def move(hop, place):
        return pltpu.make_async_remote_copy(
            src_ref=mine, dst_ref=got.at[place], send_sem=send_sem.at[hop],
            recv_sem=recv_sem.at[hop], device_id={"gx": lax.rem(me + hop, count)},
            device_id_type=pl.DeviceIdType.MESH,
        )

    for hop in range(1, count):
        move(hop, me).start()
    got[me] = local_sum
    for hop in range(1, count):
        move(hop, lax.rem(me - hop + count, count)).wait_recv()
    total = got[0]
    for place in range(1, count):
        total = total + got[place]
    q = [total[:, i : i + 1] for i in range(SUMS)]
    res_norm, rv_re, rv_im, image_sq, wr_re, wr_im, wv_re, wv_im, twice_sq = q[:9]
    half = floor_share * res_norm
    bounded = jnp.maximum(rv_re * rv_re + rv_im * rv_im, half * half)
    step_re = res_norm * rv_re / bounded
    step_im = -res_norm * rv_im / bounded
    step_sq = step_re * step_re + step_im * step_im
    ts_re = rv_re - step_re * image_sq - (step_re * wr_re + step_im * wr_im) + step_sq * wv_re
    ts_im = -rv_im - step_im * image_sq - (step_re * wr_im - step_im * wr_re) + step_sq * wv_im
    tt_sum = image_sq - 2.0 * (step_re * wv_re + step_im * wv_im) + step_sq * twice_sq
    omega_re = ts_re / tt_sum
    omega_im = ts_im / tt_sum
    found = [step_re, step_im, omega_re, omega_im]
    if with_overlap:
        mx_re, mx_im, mz_re, mz_im, my_re, my_im = q[9:15]
        ms_re = mz_re - (step_re * my_re - step_im * my_im)
        ms_im = mz_im - (step_re * my_im + step_im * my_re)
        found.append(
            mx_re + (step_re * mz_re - step_im * mz_im) + (omega_re * ms_re - omega_im * ms_im)
        )
        found.append(
            mx_im + (step_re * mz_im + step_im * mz_re) + (omega_re * ms_im + omega_im * ms_re)
        )
    lane = lax.broadcasted_iota(jnp.int32, coef.shape, 1)
    packed = jnp.zeros(coef.shape, jnp.float32)
    for i, value in enumerate(found):
        packed = jnp.where(lane == i, value, packed)
    coef[...] = packed
    for hop in range(1, count):
        move(hop, me).wait_send()


def sum_over_gx(parts, with_overlap, ident):
    count = lax.axis_size("gx")
    waves = parts.shape[0]
    return pl.pallas_call(
        functools.partial(sum_kernel, count, with_overlap),
        out_shape=jax.ShapeDtypeStruct((waves, SUMS), jnp.float32),
        in_specs=[pl.BlockSpec(memory_space=pltpu.VMEM)],
        out_specs=pl.BlockSpec(memory_space=pltpu.VMEM),
        scratch_shapes=[
            pltpu.VMEM((waves, SUMS), jnp.float32),
            pltpu.VMEM((count, waves, SUMS), jnp.float32),
            pltpu.SemaphoreType.DMA((count,)),
            pltpu.SemaphoreType.DMA((count,)),
        ],
        compiler_params=pltpu.CompilerParams(collective_id=ident, has_side_effects=True),
        name="sum_first" if with_overlap else "sum_second",
    )(parts)


def gradient_kernel(count, part_ref, mask_ref, out, got, total, spread, sems):
    me = lax.axis_index("wa")
    width = part_ref.shape[1] // count

    def columns(place):
        return pl.ds(pl.multiple_of(place * width, 128), width)

    greet("wa", count, me)

    def scatter(hop, place):
        to = lax.rem(me + hop, count)
        return pltpu.make_async_remote_copy(
            src_ref=part_ref.at[:, columns(to)], dst_ref=got.at[place],
            send_sem=sems.at[0, hop], recv_sem=sems.at[1, hop],
            device_id={"wa": to}, device_id_type=pl.DeviceIdType.MESH,
        )

    def gather(hop, place):
        return pltpu.make_async_remote_copy(
            src_ref=total, dst_ref=spread.at[place],
            send_sem=sems.at[2, hop], recv_sem=sems.at[3, hop],
            device_id={"wa": lax.rem(me + hop, count)}, device_id_type=pl.DeviceIdType.MESH,
        )

    for hop in range(1, count):
        scatter(hop, me).start()
    got[me] = part_ref[:, columns(me)]
    for hop in range(1, count):
        scatter(hop, lax.rem(me - hop + count, count)).wait_recv()
    summed = got[0]
    for place in range(1, count):
        summed = summed + got[place]
    total[...] = summed
    for hop in range(1, count):
        gather(hop, me).start()
    spread[me] = summed
    for hop in range(1, count):
        gather(hop, lax.rem(me - hop + count, count)).wait_recv()
    for place in range(count):
        span = slice(place * width, (place + 1) * width)
        out[:, span] = mask_ref[:, span].astype(jnp.float32) * spread[place]
    for hop in range(1, count):
        scatter(hop, me).wait_send()
        gather(hop, me).wait_send()


def gradient_sum(part, mask):
    count = lax.axis_size("wa")
    rows, width = part.shape
    piece = (rows, width // count)
    return pl.pallas_call(
        functools.partial(gradient_kernel, count),
        out_shape=jax.ShapeDtypeStruct(part.shape, jnp.float32),
        in_specs=[pl.BlockSpec(memory_space=pltpu.VMEM)] * 2,
        out_specs=pl.BlockSpec(memory_space=pltpu.VMEM),
        scratch_shapes=[
            pltpu.VMEM((count, *piece), jnp.float32),
            pltpu.VMEM(piece, jnp.float32),
            pltpu.VMEM((count, *piece), jnp.float32),
            pltpu.SemaphoreType.DMA((4, count)),
        ],
        compiler_params=pltpu.CompilerParams(collective_id=2, has_side_effects=True),
        name="sum_gradient",
    )(part, mask)


def neighbours(cells, dim, reach):
    count = lax.axis_size("gx")
    extent = cells.shape[dim]
    head = lax.slice_in_dim(cells, 0, reach, axis=dim)
    tail = lax.slice_in_dim(cells, extent - reach, extent, axis=dim)
    hi = lax.ppermute(head, "gx", [((i + 1) % count, i) for i in range(count)])
    lo = lax.ppermute(tail, "gx", [(i, (i + 1) % count) for i in range(count)])
    return hi, lo


def local(
    warm_field,
    warm_adjoint,
    permittivity,
    design_mask,
    source_row,
    monitor_row,
    wavenumber,
    bloch_phase,
    source_profile,
    monitor_profile,
):
    waves, _, rows, width = warm_field.shape
    total = rows + TILE
    count = lax.axis_size("gx")
    whole = rows * count
    me = lax.axis_index("gx")
    at_first, at_last = me == 0, me == count - 1
    cosine, sine = jnp.cos(bloch_phase), jnp.sin(bloch_phase)
    one, zero = jnp.ones_like(cosine), jnp.zeros_like(cosine)
    low_c = jnp.where(at_first, cosine, one)
    low_s = jnp.where(at_first, -sine, zero)
    high_c = jnp.where(at_last, cosine, one)
    high_s = jnp.where(at_last, sine, zero)

    def spot_of(row):
        away = jnp.remainder(row - me * rows, whole)
        spot = jnp.where(
            away < rows + REACH, away,
            jnp.where(away >= whole - REACH, away - whole + total, -1),
        )
        above = (spot >= rows) & (spot < rows + REACH)
        below = spot >= rows + REACH
        turn_c = jnp.where(above, high_c, jnp.where(below, low_c, one))
        turn_s = jnp.where(above, high_s, jnp.where(below, low_s, zero))
        return spot, turn_c, turn_s

    src_spot, src_c, src_s = spot_of(source_row)
    mon_spot, mon_c, mon_s = spot_of(monitor_row)
    scal = jnp.stack(
        [wavenumber, low_c, low_s, high_c, high_s, src_c, src_s, mon_c, -mon_s], axis=1
    )
    spots = jnp.stack([src_spot, mon_spot], axis=1)
    eps_hi, eps_lo = neighbours(permittivity, 0, REACH)
    eps = jnp.concatenate(
        [permittivity, eps_hi, jnp.ones((TILE - 2 * REACH, width), jnp.float32), eps_lo], axis=0
    )
    hi, lo = neighbours(warm_field, 2, REACH)
    ahi, alo = neighbours(warm_adjoint, 2, REACH)

    smem = pl.BlockSpec(memory_space=pltpu.SMEM)
    field_spec = pl.BlockSpec((1, 2, rows, width), lambda w: (w, 0, 0, 0))
    rim_spec = pl.BlockSpec((1, 2, REACH, width), lambda w: (w, 0, 0, 0))
    row_spec = pl.BlockSpec((1, 2, width), lambda w: (w, 0, 0))
    eps_spec = pl.BlockSpec((total, width), lambda w: (0, 0))
    dot_spec = pl.BlockSpec((1, SUMS, 128), lambda w: (w, 0, 0))
    grad_spec = pl.BlockSpec((rows, width), lambda w: (0, 0))
    field_shape = jax.ShapeDtypeStruct(warm_field.shape, jnp.float32)
    dot_shape = jax.ShapeDtypeStruct((waves, SUMS, 128), jnp.float32)
    ext_shape = pltpu.VMEM((2, total, width), jnp.float32)
    flat_shape = pltpu.VMEM((2, rows, width), jnp.float32)
    params = pltpu.CompilerParams(
        dimension_semantics=("arbitrary",), vmem_limit_bytes=VMEM_LIMIT
    )
    field_bytes = 4 * waves * 2 * rows * width

    def cost(ops, fields):
        return pl.CostEstimate(
            flops=ops * field_bytes // 4, bytes_accessed=fields * field_bytes, transcendentals=0
        )

    dots = pl.pallas_call(
        first_pass,
        grid=(waves,),
        out_shape=dot_shape,
        in_specs=[smem, smem, eps_spec, field_spec, rim_spec, rim_spec, row_spec, row_spec],
        out_specs=dot_spec,
        scratch_shapes=[ext_shape, ext_shape, flat_shape, flat_shape],
        compiler_params=params,
        cost_estimate=cost(60, 1),
        name="first_pass",
    )(scal, spots, eps, warm_field, hi, lo, source_profile, monitor_profile)
    coef = sum_over_gx(dots, True, 0)
    forward, adots = pl.pallas_call(
        second_pass,
        grid=(waves,),
        out_shape=(field_shape, dot_shape),
        in_specs=[smem, smem, smem, eps_spec]
        + [field_spec, rim_spec, rim_spec] * 2
        + [row_spec, row_spec],
        out_specs=(field_spec, dot_spec),
        scratch_shapes=[ext_shape] * 4,
        compiler_params=params,
        cost_estimate=cost(100, 3),
        name="second_pass",
    )(
        scal, spots, coef, eps, warm_field, hi, lo, warm_adjoint, ahi, alo,
        source_profile, monitor_profile,
    )
    acoef = sum_over_gx(adots, False, 1)
    adjoint, grad_part = pl.pallas_call(
        third_pass,
        grid=(waves,),
        out_shape=(field_shape, jax.ShapeDtypeStruct((rows, width), jnp.float32)),
        in_specs=[smem, smem, smem, smem, eps_spec, field_spec, rim_spec, rim_spec, row_spec,
                  field_spec],
        out_specs=(field_spec, grad_spec),
        scratch_shapes=[ext_shape] * 2,
        compiler_params=params,
        cost_estimate=cost(50, 3),
        name="third_pass",
    )(scal, spots, coef, acoef, eps, warm_adjoint, ahi, alo, monitor_profile, forward)
    gradient = gradient_sum(grad_part, design_mask)
    return (forward, adjoint, gradient)


def solution(mesh):
    placed = (
        P("wa", None, "gx", None),
        P("wa", None, "gx", None),
        P("gx", None),
        P("gx", None),
        P("wa"),
        P("wa"),
        P("wa"),
        P("wa"),
        P("wa", None, None),
        P("wa", None, None),
    )
    return jax.shard_map(
        local,
        mesh=mesh,
        in_specs=placed,
        out_specs=(P("wa", None, "gx", None), P("wa", None, "gx", None), P("gx", None)),
        check_vma=False,
    )
```

profile of v0, /device:TPU:0, one launch (start us, length us, event | category | flops | bytes accessed | tf_op | source)
XLA Modules:
  0.0 143.3 jit_solution(11507483047173445405)
XLA Ops:
  0.6 1.0 fusion.15
  1.7 3.4 %collective-permute-start = (f32[3,2048]{1,0:T(4,128)S(1)}, f32[3,2048]{1,0:T(4,128)S(1)}, u32[]{:S(2)}, u32[]{:S(2)}) collective-permute-start(f32[3,2048]{1,0:T(4,128)S(1)} %get-tuple-element.19), channel_id=1, source_target_pairs={{4,0},{8,4},{12,8},{16,12},{20,16},{24,20},{28,24},{0,28},{5,1},{9... | collective-permute-start | bytes 73736 | tf_op jit(solution)/shard_map/ppermute | solution.py:354
  5.1 2.7 %fusion.14 = (f32[16,2,3,2048]{3,2,1,0:T(4,128)S(1)}, f32[16,2,3,2048]{3,2,1,0:T(4,128)S(1)}) fusion(f32[16,2,16,2048]{3,2,1,0:T(8,128)} %x_ref.3), kind=kLoop, calls=%fused_computation.37 | loop fusion | bytes 3145728 | tf_op jit(solution)/shard_map/slice | solution.py:353
  7.8 0.5 copy.48
  8.3 0.7 collective-permute-start.2
  9.0 1.3 copy.49
  10.4 0.5 fusion.13
  10.9 1.3 copy.50
  12.3 2.6 %collective-permute-start.4 = (f32[16,2,3,2048]{3,0,2,1:T(8,128)}, f32[16,2,3,2048]{3,0,2,1:T(8,128)}, u32[]{:S(2)}, u32[]{:S(2)}) collective-permute-start(f32[16,2,3,2048]{3,0,2,1:T(8,128)} %copy.50), channel_id=1, source_target_pairs={{4,0},{8,4},{12,8},{16,12},{20,16},{24,20},{28,24},{0,28},{5,1},{9... | collective-permute-start | bytes 2359304 | tf_op jit(solution)/shard_map/ppermute | solution.py:354
  14.9 1.4 copy.51
  17.4 0.1 stack.48.scal
  17.5 27.6 %collective-permute-done.1 = f32[3,2048]{1,0:T(4,128)S(1)} collective-permute-done((f32[3,2048]{1,0:T(4,128)S(1)}, f32[3,2048]{1,0:T(4,128)S(1)}, u32[]{:S(2)}, u32[]{:S(2)}) %collective-permute-start.1) | collective-permute-done | bytes 24608 | tf_op jit(solution)/shard_map/ppermute | solution.py:355
  45.2 0.5 copy.36.hi_ref
  45.8 1.7 %copy.37.lo_ref = f32[16,2,3,2048]{3,2,1,0:T(4,128)S(1)} copy(f32[16,2,3,2048]{3,0,2,1:T(8,128)} %collective-permute-done.3) | data formatting | bytes 1572864 | tf_op jit(solution)/shard_map/ppermute | solution.py:355
  47.5 15.7 %first_pass.1.parts = f32[16,16,128]{2,1,0:T(8,128)S(1)} custom-call(f32[16,9]{1,0:T(8,128)S(1)} %stack.48.scal, s32[16,2]{1,0:T(8,128)S(1)} %copy.40.spots, f32[24,2048]{1,0:T(8,128)S(1)} %pad_maximum_fusion.eps, f32[16,2,16,2048]{3,2,1,0:T(8,128)} %x_ref.3, f32[16,2,3,2048]{3,2,1,0:T(4,128)S(1)} %copy.36.hi_ref, f32[16,2,3,2048]{3,2,1,0:T(4,128)S(1)} %copy.37.lo_ref, ...), custom_call_target="tpu_custom_call" | custom-call | flops 62914560 | bytes 4194304 | tf_op jit(solution)/shard_map/first_pass/pallas_call | solution.py:430
  63.2 0.6 copy-done.7
  63.8 7.1 %sum_first.1.coef = f32[16,16]{1,0:T(8,128)} custom-call(f32[16,16,128]{2,1,0:T(8,128)} %copy-done.7), custom_call_target="tpu_custom_call" | custom-call | tf_op jit(solution)/shard_map/sum_first/pallas_call | solution.py:267
  70.9 1.7 %copy.43.ahi_ref = f32[16,2,3,2048]{3,2,1,0:T(4,128)S(1)} copy(f32[16,2,3,2048]{3,0,2,1:T(8,128)} %collective-permute-done.4) | data formatting | bytes 1572864 | tf_op jit(solution)/shard_map/ppermute | solution.py:354
  72.6 1.7 %copy.44.alo_ref = f32[16,2,3,2048]{3,2,1,0:T(4,128)S(1)} copy(f32[16,2,3,2048]{3,0,2,1:T(8,128)} %collective-permute-done.5) | data formatting | bytes 1572864 | tf_op jit(solution)/shard_map/ppermute | solution.py:355
  74.3 0.9 copy-done.3
  75.2 0.9 copy-done.6
  76.2 0.7 copy-done.10
  76.9 24.2 %second_pass.1 = (f32[16,2,16,2048]{3,2,1,0:T(8,128)}, f32[16,16,128]{2,1,0:T(8,128)S(1)}) custom-call(f32[16,9]{1,0:T(8,128)S(1)} %stack.48.scal, s32[16,2]{1,0:T(8,128)S(1)} %copy.40.spots, f32[16,16]{1,0:T(8,128)S(1)} %copy-done.10, f32[24,2048]{1,0:T(8,128)S(1)} %pad_maximum_fusion.eps, f32[16,2,16,2048]{3,2,1,0:T(8,128)} %x_ref.3, ...), custom_call_target="tpu_custom_call" | custom-call | flops 104857600 | bytes 12582912 | tf_op jit(solution)/shard_map/second_pass/pallas_call | solution.py:442
  101.0 0.7 copy-done.9
  101.7 6.9 %sum_second.1.acoef = f32[16,16]{1,0:T(8,128)} custom-call(f32[16,16,128]{2,1,0:T(8,128)} %copy-done.9), custom_call_target="tpu_custom_call" | custom-call | tf_op jit(solution)/shard_map/sum_second/pallas_call | solution.py:267
  108.6 1.2 copy-done.1
  109.9 0.9 copy-done.4
  110.8 0.7 copy-done.12
  111.5 15.7 %third_pass.1 = (f32[16,2,16,2048]{3,2,1,0:T(8,128)}, f32[16,2048]{1,0:T(8,128)S(1)}) custom-call(f32[16,9]{1,0:T(8,128)S(1)} %stack.48.scal, s32[16,2]{1,0:T(8,128)S(1)} %copy.40.spots, f32[16,16]{1,0:T(8,128)S(1)} %copy-done.11, f32[16,16]{1,0:T(8,128)S(1)} %copy-done.12, f32[24,2048]{1,0:T(8,128)S(1)} %pad_maximum_fusion.eps, f32[16,2,16,2048]{3,2,1,0:T(8,128)} %ax_ref.3, ...), custom_call_target="tpu_custom_call" | custom-call | flops 52428800 | bytes 12582912 | tf_op jit(solution)/shard_map/third_pass/pallas_call | solution.py:459
  127.2 0.7 copy-done.8
  127.8 13.9 %sum_gradient.1 = f32[16,2048]{1,0:T(8,128)} custom-call(f32[16,2048]{1,0:T(8,128)} %copy-done.8, s32[16,2048]{1,0:T(8,128)} %mask_ref.1), custom_call_target="tpu_custom_call" | custom-call | tf_op jit(solution)/shard_map/sum_gradient/pallas_call | solution.py:333
  141.8 1.6 %copy.53 = f32[16,2048]{1,0:T(8,128)} copy(f32[16,2048]{1,0:T(8,128)} %sum_gradient.1) | data formatting | bytes 262144
  (54 shorter events, 1.3 us)
Async XLA Ops:
  0.6 9.8 %copy-start.13 = (f32[16,2,16,2048]{3,2,1,0:T(8,128)S(1)}, f32[16,2,16,2048]{3,2,1,0:T(8,128)}, u32[]{:S(2)}) copy-start(f32[16,2,16,2048]{3,2,1,0:T(8,128)} %ax_ref.3) | copy-start | bytes 12582916
  1.7 14.7 %collective-permute-start = (f32[3,2048]{1,0:T(4,128)S(1)}, f32[3,2048]{1,0:T(4,128)S(1)}, u32[]{:S(2)}, u32[]{:S(2)}) collective-permute-start(f32[3,2048]{1,0:T(4,128)S(1)} %get-tuple-element.19), channel_id=1, source_target_pairs={{4,0},{8,4},{12,8},{16,12},{20,16},{24,20},{28,24},{0,28},{5,1},{9... | collective-permute-start | bytes 73736 | tf_op jit(solution)/shard_map/ppermute | solution.py:354
  8.3 37.0 %collective-permute-start.2 = (f32[16,2,3,2048]{3,0,2,1:T(8,128)S(1)}, f32[16,2,3,2048]{3,0,2,1:T(8,128)S(1)}, u32[]{:S(2)}, u32[]{:S(2)}) collective-permute-start(f32[16,2,3,2048]{3,0,2,1:T(8,128)S(1)} %copy.48), channel_id=1, source_target_pairs={{4,0},{8,4},{12,8},{16,12},{20,16},{24,20},{28,24},{0,28},{5,1},{9... | collective-permute-start | bytes 2359304 | tf_op jit(solution)/shard_map/ppermute | solution.py:354
  10.3 6.0 %copy-start.18 = (f32[16]{0:T(128)S(1)}, f32[16]{0:T(128)}, u32[]{:S(2)}) copy-start(f32[16]{0:T(128)} %param.17) | copy-start | bytes 196
  10.3 6.0 %copy-start.15 = (s32[16]{0:T(128)S(1)}, s32[16]{0:T(128)}, u32[]{:S(2)}) copy-start(s32[16]{0:T(128)} %param.15) | copy-start | bytes 196
  10.3 6.0 %copy-start.16 = (s32[16]{0:T(128)S(1)}, s32[16]{0:T(128)}, u32[]{:S(2)}) copy-start(s32[16]{0:T(128)} %param.14) | copy-start | bytes 196
  10.3 6.9 %copy-start.17 = (f32[16]{0:T(128)S(1)}, f32[16]{0:T(128)}, u32[]{:S(2)}) copy-start(f32[16]{0:T(128)} %param.16) | copy-start | bytes 196
  10.3 34.8 %copy-start.14 = (f32[16,2048]{1,0:T(8,128)S(1)}, f32[16,2048]{1,0:T(8,128)}, u32[]{:S(2)}) copy-start(f32[16,2048]{1,0:T(8,128)} %param.12) | copy-start | bytes 393220
  10.3 35.4 %collective-permute-start.3 = (f32[16,2,3,2048]{3,0,2,1:T(8,128)}, f32[16,2,3,2048]{3,0,2,1:T(8,128)}, u32[]{:S(2)}, u32[]{:S(2)}) collective-permute-start(f32[16,2,3,2048]{3,0,2,1:T(8,128)} %copy.49), channel_id=1, source_target_pairs={{0,4},{4,8},{8,12},{12,16},{16,20},{20,24},{24,28},{28,0},{1,5},{5... | collective-permute-start | bytes 2359304 | tf_op jit(solution)/shard_map/ppermute | solution.py:355
  10.9 36.6 %copy-start.2 = (f32[16,2,2048]{2,1,0:T(2,128)S(1)}, f32[16,2,2048]{2,1,0:T(2,128)}, u32[]{:S(2)}) copy-start(f32[16,2,2048]{2,1,0:T(2,128)} %mon_ref.5) | copy-start | bytes 786436
  10.9 36.6 %copy-start.5 = (f32[16,2,2048]{2,1,0:T(2,128)S(1)}, f32[16,2,2048]{2,1,0:T(2,128)}, u32[]{:S(2)}) copy-start(f32[16,2,2048]{2,1,0:T(2,128)} %src_ref.3) | copy-start | bytes 786436
  12.3 58.6 %collective-permute-start.4 = (f32[16,2,3,2048]{3,0,2,1:T(8,128)}, f32[16,2,3,2048]{3,0,2,1:T(8,128)}, u32[]{:S(2)}, u32[]{:S(2)}) collective-permute-start(f32[16,2,3,2048]{3,0,2,1:T(8,128)} %copy.50), channel_id=1, source_target_pairs={{4,0},{8,4},{12,8},{16,12},{20,16},{24,20},{28,24},{0,28},{5,1},{9... | collective-permute-start | bytes 2359304 | tf_op jit(solution)/shard_map/ppermute | solution.py:354
  16.3 56.3 %collective-permute-start.5 = (f32[16,2,3,2048]{3,0,2,1:T(8,128)}, f32[16,2,3,2048]{3,0,2,1:T(8,128)}, u32[]{:S(2)}, u32[]{:S(2)}) collective-permute-start(f32[16,2,3,2048]{3,0,2,1:T(8,128)} %copy.51), channel_id=1, source_target_pairs={{0,4},{4,8},{8,12},{12,16},{16,20},{20,24},{24,28},{28,0},{1,5},{5... | collective-permute-start | bytes 2359304 | tf_op jit(solution)/shard_map/ppermute | solution.py:355
  16.4 28.7 %collective-permute-start.1 = (f32[3,2048]{1,0:T(4,128)S(1)}, f32[3,2048]{1,0:T(4,128)S(1)}, u32[]{:S(2)}, u32[]{:S(2)}) collective-permute-start(f32[3,2048]{1,0:T(4,128)S(1)} %get-tuple-element.20), channel_id=1, source_target_pairs={{0,4},{4,8},{8,12},{12,16},{16,20},{20,24},{24,28},{28,0},{1,5},{5... | collective-permute-start | bytes 73736 | tf_op jit(solution)/shard_map/ppermute | solution.py:355
  63.2 0.7 copy-start.7
  74.3 1.0 copy-start.3
  75.2 0.9 copy-start.6
  76.2 0.7 copy-start.10
  76.9 24.2 %copy-start = (f32[16,2,3,2048]{3,2,1,0:T(4,128)}, f32[16,2,3,2048]{3,2,1,0:T(4,128)S(1)}, u32[]{:S(2)}) copy-start(f32[16,2,3,2048]{3,2,1,0:T(4,128)S(1)} %copy.44.alo_ref) | copy-start | bytes 2359300
  76.9 31.7 %copy-start.11 = (f32[16,16]{1,0:T(8,128)S(1)}, f32[16,16]{1,0:T(8,128)}, u32[]{:S(2)}) copy-start(f32[16,16]{1,0:T(8,128)} %sum_first.1.coef) | copy-start | bytes 3076
  101.0 0.7 copy-start.9
  108.6 1.2 copy-start.1
  109.9 0.9 copy-start.4
  110.8 0.7 copy-start.12
  127.2 0.7 copy-start.8
where the time goes:
time: 144 us; the launch traced here: 143 us
  Pallas kernels  83.4 us (58%)
  waiting for transfers between devices  27.6 us (19%)
  local copies, waits for them, and re-layouts  24.4 us (17%)
  starting transfers between devices  6.88 us (5%)
    ppermute x3, waiting for transfers between devices, neighbours(): lo = lax.ppermute(tail, 'gx', [(i, (i + 1) % count) for i in range(count)])  27.6 us
    pallas_call x1, Pallas kernels, local(): pl.pallas_call(second_pass, grid=(waves,), out_shape=(field_shape, dot_sh...  24.2 us
    pallas_call x1, Pallas kernels, local(): pl.pallas_call(first_pass, grid=(waves,), out_shape=dot_shape, in_specs=[...  15.7 us
    pallas_call x1, Pallas kernels, local(): pl.pallas_call(third_pass, grid=(waves,), out_shape=(field_shape, jax.Sha...  15.7 us
    pallas_call x2, Pallas kernels, sum_over_gx(): pl.pallas_call(functools.partial(sum_kernel, count, with_overlap), out_sh...  14 us
    pallas_call x1, Pallas kernels, gradient_sum(): pl.pallas_call(functools.partial(gradient_kernel, count), out_shape=jax.S...  13.9 us
    unnamed x43, local copies, waits for them, and re-layouts  13.6 us
    ppermute x3, starting transfers between devices, neighbours(): hi = lax.ppermute(head, 'gx', [((i + 1) % count, i) for i in range(count)])  6.76 us
  transfers between devices with their start and end apart: 6, of which 1 were waited for; matrix products, arithmetic and copies ran while one was open for 9% of the time, Pallas kernels for 16%

commit v1 on v0

--- a/solution.py
+++ b/solution.py
@@ -11,17 +11,26 @@
 REACH = 3
 TILE = 8
 SUMS = 16
-VMEM_LIMIT = 48 * 1024 * 1024
+VMEM_LIMIT = 60 * 1024 * 1024
+
+
+def edge_free(u, step):
+    width = u.shape[1]
+    turned = pltpu.roll(u, step % width, 1)
+    lane = lax.broadcasted_iota(jnp.int32, (u.shape[0], 128), 1)
+    if step < 0:
+        end = jnp.where(lane == 127, 0.0, turned[:, width - 128 :])
+        return jnp.concatenate([turned[:, : width - 128], end], axis=1)
+    end = jnp.where(lane == 0, 0.0, turned[:, :128])
+    return jnp.concatenate([end, turned[:, 128:]], axis=1)
 
 
 def stencil(u, d, rows):
-    total, width = u.shape
-    col = lax.broadcasted_iota(jnp.int32, (total, width), 1)
-    after = jnp.where(col == width - 1, 0.0, pltpu.roll(u, width - 1, 1))
-    before = jnp.where(col == 0, 0.0, pltpu.roll(u, 1, 1))
-    above = pltpu.roll(u, total - 1, 0)
-    below = pltpu.roll(u, 1, 0)
-    return (d * u - (above + below + after + before))[:rows]
+    total = u.shape[0]
+    above = pltpu.roll(u, total - 1, 0)[:rows]
+    below = pltpu.roll(u, 1, 0)[:rows]
+    u = u[:rows]
+    return d[:rows] * u - (above + below + edge_free(u, -1) + edge_free(u, 1))
 
 
 def lay_out(ext, x_ref, hi_ref, lo_ref, scal, wave, sign):
@@ -346,11 +355,15 @@
     )(part, mask)
 
 
-def neighbours(cells, dim, reach):
-    count = lax.axis_size("gx")
+def ends(cells, dim, reach):
     extent = cells.shape[dim]
     head = lax.slice_in_dim(cells, 0, reach, axis=dim)
     tail = lax.slice_in_dim(cells, extent - reach, extent, axis=dim)
+    return head, tail
+
+
+def neighbours(head, tail):
+    count = lax.axis_size("gx")
     hi = lax.ppermute(head, "gx", [((i + 1) % count, i) for i in range(count)])
     lo = lax.ppermute(tail, "gx", [(i, (i + 1) % count) for i in range(count)])
     return hi, lo
@@ -399,12 +412,14 @@
         [wavenumber, low_c, low_s, high_c, high_s, src_c, src_s, mon_c, -mon_s], axis=1
     )
     spots = jnp.stack([src_spot, mon_spot], axis=1)
-    eps_hi, eps_lo = neighbours(permittivity, 0, REACH)
+    eps_hi, eps_lo = neighbours(*ends(permittivity, 0, REACH))
     eps = jnp.concatenate(
         [permittivity, eps_hi, jnp.ones((TILE - 2 * REACH, width), jnp.float32), eps_lo], axis=0
     )
-    hi, lo = neighbours(warm_field, 2, REACH)
-    ahi, alo = neighbours(warm_adjoint, 2, REACH)
+    hi, lo = neighbours(*ends(warm_field, 2, REACH))
+    adj_head, adj_tail = ends(warm_adjoint, 2, REACH)
+    adj_head, adj_tail, hi, lo = lax.optimization_barrier((adj_head, adj_tail, hi, lo))
+    ahi, alo = neighbours(adj_head, adj_tail)
 
     smem = pl.BlockSpec(memory_space=pltpu.SMEM)
     field_spec = pl.BlockSpec((1, 2, rows, width), lambda w: (w, 0, 0, 0))

time: 144 us -> 133 us (0.924)
  waiting for transfers between devices: 27.6 us -> 13.1 us
  Pallas kernels: 83.4 us -> 86.4 us
  local copies, waits for them, and re-layouts: 24.4 us -> 22 us
  starting transfers between devices: 6.88 us -> 8.36 us
    ppermute x3, waiting for transfers between devices: 27.6 us -> 0.47 us  [neighbours(): lo = lax.ppermute(tail, 'gx', [(i, (i + 1) % count) for i in range(count)])]
    ppermute x3, waiting for transfers between devices: 0.01 us -> 12.7 us  [neighbours(): hi = lax.ppermute(head, 'gx', [((i + 1) % count, i) for i in range(count)])]
    unnamed x43 -> x13, local copies, waits for them, and re-layouts: 13.6 us -> 4.27 us
    optimization_barrier x0 -> x4, local copies, waits for them, and re-layouts: none -> 3.94 us  [local(): lax.optimization_barrier((adj_head, adj_tail, hi, lo))]
    slice x3, local copies, waits for them, and re-layouts: 4.2 us -> 6.29 us  [the longest x2 5.41 us: ends(): tail = lax.slice_in_dim(cells, extent - reach, extent, axis=dim)]
    ppermute x3, starting transfers between devices: 6.76 us -> 8.29 us  [neighbours(): hi = lax.ppermute(head, 'gx', [((i + 1) % count, i) for i in range(count)])]
    ppermute x2 -> x1, local copies, waits for them, and re-layouts: 3.36 us -> 2.67 us  [neighbours(): lo = lax.ppermute(tail, 'gx', [(i, (i + 1) % count) for i in range(count)])]
  transfers between devices with their start and end apart: 6 -> 6, of which waited for: 1 -> 2; matrix products, arithmetic and copies ran while one was open for 9% -> 13% of each run, Pallas kernels for 16% -> 18%
where the time goes in v1:
time: 133 us; the launch traced here: 132 us
  Pallas kernels  86.4 us (65%)
  local copies, waits for them, and re-layouts  22 us (17%)
  waiting for transfers between devices  13.1 us (10%)
  starting transfers between devices  8.36 us (6%)
    pallas_call x1, Pallas kernels, local(): pl.pallas_call(second_pass, grid=(waves,), out_shape=(field_shape, dot_sh...  24.6 us
    pallas_call x1, Pallas kernels, local(): pl.pallas_call(first_pass, grid=(waves,), out_shape=dot_shape, in_specs=[...  17.1 us
    pallas_call x1, Pallas kernels, local(): pl.pallas_call(third_pass, grid=(waves,), out_shape=(field_shape, jax.Sha...  16.6 us
    pallas_call x2, Pallas kernels, sum_over_gx(): pl.pallas_call(functools.partial(sum_kernel, count, with_overlap), out_sh...  14.1 us
    pallas_call x1, Pallas kernels, gradient_sum(): pl.pallas_call(functools.partial(gradient_kernel, count), out_shape=jax.S...  14 us
    ppermute x3, waiting for transfers between devices, neighbours(): hi = lax.ppermute(head, 'gx', [((i + 1) % count, i) for i in range(count)])  12.7 us
    ppermute x3, starting transfers between devices, neighbours(): hi = lax.ppermute(head, 'gx', [((i + 1) % count, i) for i in range(count)])  8.29 us
    slice x2, local copies, waits for them, and re-layouts, ends(): tail = lax.slice_in_dim(cells, extent - reach, extent, axis=dim)  5.41 us
  transfers between devices with their start and end apart: 6, of which 2 were waited for; matrix products, arithmetic and copies ran while one was open for 13% of the time, Pallas kernels for 18%

profile of v1, /device:TPU:0, one launch (start us, length us, event | category | flops | bytes accessed | tf_op | source)
XLA Modules:
  0.0 131.6 jit_solution(5749440332216934063)
XLA Ops:
  0.6 0.9 fusion.15
  1.5 3.4 %collective-permute-start = (f32[3,2048]{1,0:T(4,128)S(1)}, f32[3,2048]{1,0:T(4,128)S(1)}, u32[]{:S(2)}, u32[]{:S(2)}) collective-permute-start(f32[3,2048]{1,0:T(4,128)S(1)} %get-tuple-element.27), channel_id=1, source_target_pairs={{4,0},{8,4},{12,8},{16,12},{20,16},{24,20},{28,24},{0,28},{5,1},{9... | collective-permute-start | bytes 73736 | tf_op jit(solution)/shard_map/ppermute | solution.py:367
  4.9 2.7 %fusion.13 = (f32[16,2,3,2048]{3,2,1,0:T(4,128)S(1)}, f32[16,2,3,2048]{3,2,1,0:T(4,128)S(1)}) fusion(f32[16,2,16,2048]{3,2,1,0:T(8,128)} %x_ref.3), kind=kLoop, calls=%fused_computation.36 | loop fusion | bytes 3145728 | tf_op jit(solution)/shard_map/slice | solution.py:361
  7.6 1.3 %copy.50 = f32[16,2,3,2048]{3,0,2,1:T(8,128)} copy(f32[16,2,3,2048]{3,2,1,0:T(4,128)S(1)} %get-tuple-element.24) | data formatting | bytes 1572864
  9.0 2.6 %collective-permute-start.2 = (f32[16,2,3,2048]{3,0,2,1:T(8,128)}, f32[16,2,3,2048]{3,0,2,1:T(8,128)S(1)}, u32[]{:S(2)}, u32[]{:S(2)}) collective-permute-start(f32[16,2,3,2048]{3,0,2,1:T(8,128)} %copy.50), channel_id=1, source_target_pairs={{4,0},{8,4},{12,8},{16,12},{20,16},{24,20},{28,24},{0,28},{5,1},{9... | collective-permute-start | bytes 2359304 | tf_op jit(solution)/shard_map/ppermute | solution.py:367
  11.6 1.3 %copy.51 = f32[16,2,3,2048]{3,0,2,1:T(8,128)} copy(f32[16,2,3,2048]{3,2,1,0:T(4,128)S(1)} %get-tuple-element.23) | data formatting | bytes 1572864
  13.0 2.7 %fusion.14 = (f32[16,2,3,2048]{3,2,1,0:T(4,128)S(1)}, f32[16,2,3,2048]{3,2,1,0:T(4,128)S(1)}) fusion(f32[16,2,16,2048]{3,2,1,0:T(8,128)} %ax_ref.3), kind=kLoop, calls=%fused_computation.37 | loop fusion | bytes 3145728 | tf_op jit(solution)/shard_map/slice | solution.py:361
  15.8 0.5 copy.49
  16.2 0.5 copy.48
  16.8 12.7 %collective-permute-done.2 = f32[16,2,3,2048]{3,0,2,1:T(8,128)S(1)} collective-permute-done((f32[16,2,3,2048]{3,0,2,1:T(8,128)}, f32[16,2,3,2048]{3,0,2,1:T(8,128)S(1)}, u32[]{:S(2)}, u32[]{:S(2)}) %collective-permute-start.2) | collective-permute-done | bytes 786464 | tf_op jit(solution)/shard_map/ppermute | solution.py:367
  29.5 0.5 collective-permute-done.3
  29.9 2.2 %collective-permute-start.4 = (f32[16,2,3,2048]{3,0,2,1:T(8,128)S(1)}, f32[16,2,3,2048]{3,0,2,1:T(8,128)}, u32[]{:S(2)}, u32[]{:S(2)}) collective-permute-start(f32[16,2,3,2048]{3,0,2,1:T(8,128)S(1)} %copy.48), channel_id=1, source_target_pairs={{4,0},{8,4},{12,8},{16,12},{20,16},{24,20},{28,24},{0,28},{5,1},{9... | collective-permute-start | bytes 2359304 | tf_op jit(solution)/shard_map/ppermute | solution.py:367
  32.2 0.7 copy.40.spots
  32.9 0.1 copy.31
  33.0 0.1 copy.32
  33.0 0.1 copy.29
  33.1 0.1 copy.27
  33.2 0.1 copy.25
  33.5 0.1 copy.24
  33.7 0.7 stack.48.scal
  34.4 0.7 pad_maximum_fusion.eps
  35.1 1.5 %copy.38.hi_ref = f32[16,2,3,2048]{3,2,1,0:T(4,128)} copy(f32[16,2,3,2048]{3,0,2,1:T(8,128)S(1)} %collective-permute-done.2) | data formatting | bytes 1572864 | tf_op jit(solution)/shard_map/optimization_barrier | solution.py:421
  36.7 1.5 %copy.39.lo_ref = f32[16,2,3,2048]{3,2,1,0:T(4,128)} copy(f32[16,2,3,2048]{3,0,2,1:T(8,128)S(1)} %collective-permute-done.3) | data formatting | bytes 1572864 | tf_op jit(solution)/shard_map/optimization_barrier | solution.py:421
  38.2 17.1 %first_pass.1.parts = f32[16,16,128]{2,1,0:T(8,128)} custom-call(f32[16,9]{1,0:T(8,128)} %stack.48.scal, s32[16,2]{1,0:T(8,128)} %copy.40.spots, f32[24,2048]{1,0:T(8,128)} %pad_maximum_fusion.eps, f32[16,2,16,2048]{3,2,1,0:T(8,128)} %x_ref.3, f32[16,2,3,2048]{3,2,1,0:T(4,128)} %copy.38.hi_ref, f32[16,2,3,2048]{3,2,1,0:T(4,128)} %copy.39.lo_ref, ...), custom_call_target="tpu_custom_call" | custom-call | flops 62914560 | bytes 4194304 | tf_op jit(solution)/shard_map/first_pass/pallas_call | solution.py:445
  55.2 7.3 %sum_first.1.coef = f32[16,16]{1,0:T(8,128)} custom-call(f32[16,16,128]{2,1,0:T(8,128)} %first_pass.1.parts), custom_call_target="tpu_custom_call" | custom-call | tf_op jit(solution)/shard_map/sum_first/pallas_call | solution.py:276
  62.5 2.7 %copy.43.ahi_ref = f32[16,2,3,2048]{3,2,1,0:T(4,128)} copy(f32[16,2,3,2048]{3,0,2,1:T(8,128)} %collective-permute-done.4) | data formatting | bytes 1572864 | tf_op jit(solution)/shard_map/ppermute | solution.py:367
  65.2 2.7 %copy.44.alo_ref = f32[16,2,3,2048]{3,2,1,0:T(4,128)} copy(f32[16,2,3,2048]{3,0,2,1:T(8,128)} %collective-permute-done.5) | data formatting | bytes 1572864 | tf_op jit(solution)/shard_map/ppermute | solution.py:368
  67.8 24.6 %second_pass.1 = (f32[16,2,16,2048]{3,2,1,0:T(8,128)}, f32[16,16,128]{2,1,0:T(8,128)}) custom-call(f32[16,9]{1,0:T(8,128)} %stack.48.scal, s32[16,2]{1,0:T(8,128)} %copy.40.spots, f32[16,16]{1,0:T(8,128)} %sum_first.1.coef, f32[24,2048]{1,0:T(8,128)} %pad_maximum_fusion.eps, f32[16,2,16,2048]{3,2,1,0:T(8,128)} %x_ref.3, f32[16,2,3,2048]{3,2,1,0:T(4,128)} %copy.38.hi_ref, ...), custom_call_target="tpu_custom_call" | custom-call | flops 104857600 | bytes 12582912 | tf_op jit(solution)/shard_map/second_pass/pallas_call | solution.py:457
  92.5 6.9 %sum_second.1.acoef = f32[16,16]{1,0:T(8,128)} custom-call(f32[16,16,128]{2,1,0:T(8,128)} %get-tuple-element.16.parts), custom_call_target="tpu_custom_call" | custom-call | tf_op jit(solution)/shard_map/sum_second/pallas_call | solution.py:276
  99.4 16.6 %third_pass.1 = (f32[16,2,16,2048]{3,2,1,0:T(8,128)}, f32[16,2048]{1,0:T(8,128)}) custom-call(f32[16,9]{1,0:T(8,128)} %stack.48.scal, s32[16,2]{1,0:T(8,128)} %copy.40.spots, f32[16,16]{1,0:T(8,128)} %sum_first.1.coef, f32[16,16]{1,0:T(8,128)} %sum_second.1.acoef, f32[24,2048]{1,0:T(8,128)} %pad_maximum_fusion.eps, f32[16,2,16,2048]{3,2,1,0:T(8,128)} %ax_ref.3, ...), custom_call_target="tpu_custom_call" | custom-call | flops 52428800 | bytes 12582912 | tf_op jit(solution)/shard_map/third_pass/pallas_call | solution.py:474
  115.9 14.0 %sum_gradient.1 = f32[16,2048]{1,0:T(8,128)} custom-call(f32[16,2048]{1,0:T(8,128)} %get-tuple-element.18.part_ref, s32[16,2048]{1,0:T(8,128)} %mask_ref.1), custom_call_target="tpu_custom_call" | custom-call | tf_op jit(solution)/shard_map/sum_gradient/pallas_call | solution.py:342
  130.0 1.6 %copy.53 = f32[16,2048]{1,0:T(8,128)} copy(f32[16,2048]{1,0:T(8,128)} %sum_gradient.1) | data formatting | bytes 262144
  (26 shorter events, 0.5 us)
Async XLA Ops:
  1.5 32.9 %collective-permute-start = (f32[3,2048]{1,0:T(4,128)S(1)}, f32[3,2048]{1,0:T(4,128)S(1)}, u32[]{:S(2)}, u32[]{:S(2)}) collective-permute-start(f32[3,2048]{1,0:T(4,128)S(1)} %get-tuple-element.27), channel_id=1, source_target_pairs={{4,0},{8,4},{12,8},{16,12},{20,16},{24,20},{28,24},{0,28},{5,1},{9... | collective-permute-start | bytes 73736 | tf_op jit(solution)/shard_map/ppermute | solution.py:367
  4.9 29.5 %collective-permute-start.1 = (f32[3,2048]{1,0:T(4,128)S(1)}, f32[3,2048]{1,0:T(4,128)S(1)}, u32[]{:S(2)}, u32[]{:S(2)}) collective-permute-start(f32[3,2048]{1,0:T(4,128)S(1)} %get-tuple-element.28), channel_id=1, source_target_pairs={{0,4},{4,8},{8,12},{12,16},{16,20},{20,24},{24,28},{28,0},{1,5},{5... | collective-permute-start | bytes 73736 | tf_op jit(solution)/shard_map/ppermute | solution.py:368
  9.0 20.5 %collective-permute-start.2 = (f32[16,2,3,2048]{3,0,2,1:T(8,128)}, f32[16,2,3,2048]{3,0,2,1:T(8,128)S(1)}, u32[]{:S(2)}, u32[]{:S(2)}) collective-permute-start(f32[16,2,3,2048]{3,0,2,1:T(8,128)} %copy.50), channel_id=1, source_target_pairs={{4,0},{8,4},{12,8},{16,12},{20,16},{24,20},{28,24},{0,28},{5,1},{9... | collective-permute-start | bytes 2359304 | tf_op jit(solution)/shard_map/ppermute | solution.py:367
  13.0 3.8 %copy-start.4 = (f32[16]{0:T(128)S(1)}, f32[16]{0:T(128)}, u32[]{:S(2)}) copy-start(f32[16]{0:T(128)} %param.17) | copy-start | bytes 196
  13.0 3.8 %copy-start.1 = (s32[16]{0:T(128)S(1)}, s32[16]{0:T(128)}, u32[]{:S(2)}) copy-start(s32[16]{0:T(128)} %param.15) | copy-start | bytes 196
  13.0 3.8 %copy-start.2 = (s32[16]{0:T(128)S(1)}, s32[16]{0:T(128)}, u32[]{:S(2)}) copy-start(s32[16]{0:T(128)} %param.14) | copy-start | bytes 196
  13.0 20.6 %copy-start.3 = (f32[16]{0:T(128)S(1)}, f32[16]{0:T(128)}, u32[]{:S(2)}) copy-start(f32[16]{0:T(128)} %param.16) | copy-start | bytes 196
  13.0 21.4 %copy-start = (f32[16,2048]{1,0:T(8,128)S(1)}, f32[16,2048]{1,0:T(8,128)}, u32[]{:S(2)}) copy-start(f32[16,2048]{1,0:T(8,128)} %param.12) | copy-start | bytes 393220
  13.0 17.0 %collective-permute-start.3 = (f32[16,2,3,2048]{3,0,2,1:T(8,128)}, f32[16,2,3,2048]{3,0,2,1:T(8,128)S(1)}, u32[]{:S(2)}, u32[]{:S(2)}) collective-permute-start(f32[16,2,3,2048]{3,0,2,1:T(8,128)} %copy.51), channel_id=1, source_target_pairs={{0,4},{4,8},{8,12},{12,16},{16,20},{20,24},{24,28},{28,0},{1,5},{5... | collective-permute-start | bytes 2359304 | tf_op jit(solution)/shard_map/ppermute | solution.py:368
  29.9 32.5 %collective-permute-start.4 = (f32[16,2,3,2048]{3,0,2,1:T(8,128)S(1)}, f32[16,2,3,2048]{3,0,2,1:T(8,128)}, u32[]{:S(2)}, u32[]{:S(2)}) collective-permute-start(f32[16,2,3,2048]{3,0,2,1:T(8,128)S(1)} %copy.48), channel_id=1, source_target_pairs={{4,0},{8,4},{12,8},{16,12},{20,16},{24,20},{28,24},{0,28},{5,1},{9... | collective-permute-start | bytes 2359304 | tf_op jit(solution)/shard_map/ppermute | solution.py:367
  32.2 33.0 %collective-permute-start.5 = (f32[16,2,3,2048]{3,0,2,1:T(8,128)S(1)}, f32[16,2,3,2048]{3,0,2,1:T(8,128)}, u32[]{:S(2)}, u32[]{:S(2)}) collective-permute-start(f32[16,2,3,2048]{3,0,2,1:T(8,128)S(1)} %copy.49), channel_id=1, source_target_pairs={{0,4},{4,8},{8,12},{12,16},{16,20},{20,24},{24,28},{28,0},{1,5},{5... | collective-permute-start | bytes 2359304 | tf_op jit(solution)/shard_map/ppermute | solution.py:368
